TPU v7x, 8 devices: a whole 2x2x1 slice. The times are simulated.
8 devices in a mesh: parts: 1 (over z), col: 2 (over y), row: 2 (over x), sub: 2 (over core).
Axes of the slice: x: 2, y: 2, z: 1, core: 2. Of those that a mesh axis runs over, the one named last changes fastest.
Arguments:
- edge_dist: float32 [8, 128, 1024], P(('parts', 'row', 'sub'), None, 'col')
Outputs:
- output: float32 [8, 128, 1024], P(('parts', 'row', 'sub'), None, 'col')
All inputs are finite; a program needn't handle non-finite values.
Results may differ from a plain program's by a relative error of at most 0.001.
Values sent between devices are 32-bit elements.
A program may use at most 1 GiB of HBM per device.

v0:
```python
import jax
import jax.numpy as jnp
from jax import lax
from jax.sharding import PartitionSpec as P


def close_block(block_in):
    last_axis = block_in.ndim - 1
    def pivot_step(pivot_idx, current):
        col_vec = lax.dynamic_slice_in_dim(current, pivot_idx, 1, axis=last_axis)
        row_vec = lax.dynamic_slice_in_dim(current, pivot_idx, 1, axis=last_axis - 1)
        return jnp.minimum(current, col_vec + row_vec)
    return lax.fori_loop(0, block_in.shape[-1], pivot_step, block_in)


def min_plus(left_mat, right_mat):
    return jnp.min(jnp.expand_dims(left_mat, -1) + jnp.expand_dims(right_mat, -3), axis=-2)


def solution(mesh):
    row_devs = mesh.shape['row'] * mesh.shape['sub']
    col_devs = mesh.shape['col']
    sub_devs = mesh.shape['sub']
    dist_spec = P(('parts', 'row', 'sub'), None, 'col')

    def local_run(local_dist):
        rows_local, blk_size, cols_width = local_dist.shape
        rounds = rows_local * row_devs
        my_row = lax.axis_index('row') * sub_devs + lax.axis_index('sub')
        my_col = lax.axis_index('col')
        current = local_dist
        for round_idx in range(rounds):
            in_row = my_row == round_idx % row_devs
            in_col = my_col == round_idx % col_devs
            row_pos = round_idx // row_devs
            col_pos = (round_idx // col_devs) * blk_size
            diag_blk = close_block(current[row_pos, :, col_pos:col_pos + blk_size])
            diag_blk = lax.pmin(jnp.where(in_row & in_col, diag_blk, jnp.inf), ('row', 'sub', 'col'))
            row_pan = min_plus(diag_blk, current[row_pos])
            row_pan = lax.pmin(jnp.where(in_row, row_pan, jnp.inf), ('row', 'sub'))
            col_pan = min_plus(current[:, :, col_pos:col_pos + blk_size], diag_blk)
            col_pan = lax.pmin(jnp.where(in_col, col_pan, jnp.inf), 'col')
            current = jnp.minimum(current, min_plus(col_pan, row_pan))
        return current

    return jax.shard_map(local_run, mesh=mesh, in_specs=(dist_spec,), out_specs=dist_spec, check_vma=False)
```

profile of v0, /device:TPU:1, one launch (start us, length us, event | category | flops | bytes accessed | tf_op | source)
XLA Modules:
  0.0 1249.9 jit_solution(2196357853920620348)
XLA Ops:
  7.5 38.6 %while.104 = (s32[]{:T(128)}, f32[128,128]{1,0:T(8,128)S(1)}, s32[]{:T(128)}) while((s32[]{:T(128)}, f32[128,128]{1,0:T(8,128)S(1)}, s32[]{:T(128)}) %tuple.189), condition=%wide.region_1.0_spmd, body=%wide.region_0.0_spmd.sunk | while | flops 32770 | bytes 134197 | solution.py:13
  46.8 43.1 %all-reduce.25.cloned.1.call-done = f32[128,128]{1,0:T(8,128)} async-done(((f32[128,128]{1,0:T(8,128)}), f32[128,128]{1,0:T(8,128)}) %all-reduce.25.cloned.1.call-update) | async-done | bytes 65552 | tf_op jit(solution)/shard_map/pmin | solution.py:38
  165.2 38.6 %while.105 = (s32[]{:T(128)}, f32[128,128]{1,0:T(8,128)S(1)}, s32[]{:T(128)}) while((s32[]{:T(128)}, f32[128,128]{1,0:T(8,128)S(1)}, s32[]{:T(128)}) %tuple.192), condition=%wide.region_9.10_spmd, body=%wide.region_8.9_spmd.sunk | while | flops 32770 | bytes 134197 | solution.py:13
  204.6 41.7 %all-reduce.31.cloned.1.call-done = f32[128,128]{1,0:T(8,128)} async-done(((f32[128,128]{1,0:T(8,128)}), f32[128,128]{1,0:T(8,128)}) %all-reduce.31.cloned.1.call-update) | async-done | bytes 65552 | tf_op jit(solution)/shard_map/pmin | solution.py:38
  269.2 27.8 %all-reduce.35.cloned.1.call-done = f32[128,512]{1,0:T(8,128)} async-done(((f32[128,512]{1,0:T(8,128)}), f32[128,512]{1,0:T(8,128)}) %all-reduce.35.cloned.1.call-update) | async-done | bytes 262160 | tf_op jit(solution)/shard_map/pmin | solution.py:40
  318.1 38.6 %while.106 = (s32[]{:T(128)}, f32[128,128]{1,0:T(8,128)S(1)}, s32[]{:T(128)}) while((s32[]{:T(128)}, f32[128,128]{1,0:T(8,128)S(1)}, s32[]{:T(128)}) %tuple.195), condition=%wide.region_17.18_spmd, body=%wide.region_16.17_spmd.sunk | while | flops 32770 | bytes 134197 | solution.py:13
  357.4 42.8 %all-reduce.37.cloned.1.call-done = f32[128,128]{1,0:T(8,128)} async-done(((f32[128,128]{1,0:T(8,128)}), f32[128,128]{1,0:T(8,128)}) %all-reduce.37.cloned.1.call-update) | async-done | bytes 65552 | tf_op jit(solution)/shard_map/pmin | solution.py:38
  423.2 27.9 %all-reduce.41.cloned.1.call-done = f32[128,512]{1,0:T(8,128)} async-done(((f32[128,512]{1,0:T(8,128)}), f32[128,512]{1,0:T(8,128)}) %all-reduce.41.cloned.1.call-update) | async-done | bytes 262160 | tf_op jit(solution)/shard_map/pmin | solution.py:40
  472.2 38.6 %while.107 = (s32[]{:T(128)}, f32[128,128]{1,0:T(8,128)S(1)}, s32[]{:T(128)}) while((s32[]{:T(128)}, f32[128,128]{1,0:T(8,128)S(1)}, s32[]{:T(128)}) %tuple.198), condition=%wide.region_25.26_spmd, body=%wide.region_24.25_spmd.sunk | while | flops 32770 | bytes 134197 | solution.py:13
  511.6 42.8 %all-reduce.43.cloned.1.call-done = f32[128,128]{1,0:T(8,128)} async-done(((f32[128,128]{1,0:T(8,128)}), f32[128,128]{1,0:T(8,128)}) %all-reduce.43.cloned.1.call-update) | async-done | bytes 65552 | tf_op jit(solution)/shard_map/pmin | solution.py:38
  577.3 27.8 %all-reduce.47.cloned.1.call-done = f32[128,512]{1,0:T(8,128)} async-done(((f32[128,512]{1,0:T(8,128)}), f32[128,512]{1,0:T(8,128)}) %all-reduce.47.cloned.1.call-update) | async-done | bytes 262160 | tf_op jit(solution)/shard_map/pmin | solution.py:40
  626.2 38.6 %while.108 = (s32[]{:T(128)}, f32[128,128]{1,0:T(8,128)S(1)}, s32[]{:T(128)}) while((s32[]{:T(128)}, f32[128,128]{1,0:T(8,128)S(1)}, s32[]{:T(128)}) %tuple.201), condition=%wide.region_33.34_spmd, body=%wide.region_32.33_spmd.sunk | while | flops 32770 | bytes 134197 | solution.py:13
  665.6 42.8 %all-reduce.49.cloned.1.call-done = f32[128,128]{1,0:T(8,128)} async-done(((f32[128,128]{1,0:T(8,128)}), f32[128,128]{1,0:T(8,128)}) %all-reduce.49.cloned.1.call-update) | async-done | bytes 65552 | tf_op jit(solution)/shard_map/pmin | solution.py:38
  731.3 27.8 %all-reduce.53.cloned.1.call-done = f32[128,512]{1,0:T(8,128)} async-done(((f32[128,512]{1,0:T(8,128)}), f32[128,512]{1,0:T(8,128)}) %all-reduce.53.cloned.1.call-update) | async-done | bytes 262160 | tf_op jit(solution)/shard_map/pmin | solution.py:40
  759.1 21.0 %add_reduce_fusion.3 = f32[2,128,512]{2,1,0:T(8,128)S(1)} fusion(f32[128,512]{1,0:T(8,128)} %all-reduce.53.cloned.1.call-done, f32[2,128,128]{2,1,0:T(8,128)} %all-reduce.51.cloned.1.call-done), kind=kLoop, calls=%fused_computation.35 | loop fusion | flops 33423360 | bytes 917504 | tf_op jit(solution)/shard_map/reduce_min | solution.py:17
  780.2 38.6 %while.109 = (s32[]{:T(128)}, f32[128,128]{1,0:T(8,128)S(1)}, s32[]{:T(128)}) while((s32[]{:T(128)}, f32[128,128]{1,0:T(8,128)S(1)}, s32[]{:T(128)}) %tuple.204), condition=%wide.region_41.42_spmd, body=%wide.region_40.41_spmd.sunk | while | flops 32770 | bytes 134197 | solution.py:13
  819.6 42.8 %all-reduce.55.cloned.1.call-done = f32[128,128]{1,0:T(8,128)} async-done(((f32[128,128]{1,0:T(8,128)}), f32[128,128]{1,0:T(8,128)}) %all-reduce.55.cloned.1.call-update) | async-done | bytes 65552 | tf_op jit(solution)/shard_map/pmin | solution.py:38
  885.3 27.8 %all-reduce.59.cloned.1.call-done = f32[128,512]{1,0:T(8,128)} async-done(((f32[128,512]{1,0:T(8,128)}), f32[128,512]{1,0:T(8,128)}) %all-reduce.59.cloned.1.call-update) | async-done | bytes 262160 | tf_op jit(solution)/shard_map/pmin | solution.py:40
  934.2 38.6 %while.110 = (s32[]{:T(128)}, f32[128,128]{1,0:T(8,128)S(1)}, s32[]{:T(128)}) while((s32[]{:T(128)}, f32[128,128]{1,0:T(8,128)S(1)}, s32[]{:T(128)}) %tuple.207), condition=%wide.region_49.50_spmd, body=%wide.region_48.49_spmd.sunk | while | flops 32770 | bytes 134197 | solution.py:13
  973.5 42.8 %all-reduce.61.cloned.1.call-done = f32[128,128]{1,0:T(8,128)} async-done(((f32[128,128]{1,0:T(8,128)}), f32[128,128]{1,0:T(8,128)}) %all-reduce.61.cloned.1.call-update) | async-done | bytes 65552 | tf_op jit(solution)/shard_map/pmin | solution.py:38
  1039.3 27.9 %all-reduce.65.cloned.1.call-done = f32[128,512]{1,0:T(8,128)} async-done(((f32[128,512]{1,0:T(8,128)}), f32[128,512]{1,0:T(8,128)}) %all-reduce.65.cloned.1.call-update) | async-done | bytes 262160 | tf_op jit(solution)/shard_map/pmin | solution.py:40
  1088.3 38.6 %while.111 = (s32[]{:T(128)}, f32[128,128]{1,0:T(8,128)S(1)}, s32[]{:T(128)}) while((s32[]{:T(128)}, f32[128,128]{1,0:T(8,128)S(1)}, s32[]{:T(128)}) %tuple.210), condition=%wide.region_57.58_spmd, body=%wide.region_56.57_spmd.sunk | while | flops 32770 | bytes 134197 | solution.py:13
  1127.7 42.8 %all-reduce.67.cloned.1.call-done = f32[128,128]{1,0:T(8,128)} async-done(((f32[128,128]{1,0:T(8,128)}), f32[128,128]{1,0:T(8,128)}) %all-reduce.67.cloned.1.call-update) | async-done | bytes 65552 | tf_op jit(solution)/shard_map/pmin | solution.py:38
  1193.4 27.8 %all-reduce.71.cloned.1.call-done = f32[128,512]{1,0:T(8,128)} async-done(((f32[128,512]{1,0:T(8,128)}), f32[128,512]{1,0:T(8,128)}) %all-reduce.71.cloned.1.call-update) | async-done | bytes 262160 | tf_op jit(solution)/shard_map/pmin | solution.py:40
  (3229 shorter events, 642.3 us)
Async XLA Ops:
  6.5 83.4 %all-reduce.25.cloned.1.call-start = ((), (), s32[]{:S(2)}) async-start(), calls=%async_computation | async-start | bytes 131072 | tf_op jit(solution)/shard_map/pmin | solution.py:38
  46.7 78.1 %all-reduce.29.cloned.1.call-start = ((), (), s32[]{:S(2)}) async-start(), calls=%async_computation.2 | async-start | bytes 524288 | tf_op jit(solution)/shard_map/pmin | solution.py:40
  99.3 44.8 %all-reduce.27.cloned.1.call-start = ((), (), s32[]{:S(2)}) async-start(), calls=%async_computation.1 | async-start | bytes 262144 | tf_op jit(solution)/shard_map/pmin | solution.py:42
  105.8 140.5 %all-reduce.31.cloned.1.call-start = ((), (), s32[]{:S(2)}) async-start(), calls=%async_computation.3 | async-start | bytes 131072 | tf_op jit(solution)/shard_map/pmin | solution.py:38
  204.5 64.7 %all-reduce.33.cloned.1.call-start = ((), (), s32[]{:S(2)}) async-start(), calls=%async_computation.4 | async-start | bytes 262144 | tf_op jit(solution)/shard_map/pmin | solution.py:42
  253.4 43.6 %all-reduce.35.cloned.1.call-start = ((), (), s32[]{:S(2)}) async-start(), calls=%async_computation.5 | async-start | bytes 524288 | tf_op jit(solution)/shard_map/pmin | solution.py:40
  262.0 138.3 %all-reduce.37.cloned.1.call-start = ((), (), s32[]{:S(2)}) async-start(), calls=%async_computation.6 | async-start | bytes 131072 | tf_op jit(solution)/shard_map/pmin | solution.py:38
  357.3 65.8 %all-reduce.39.cloned.1.call-start = ((), (), s32[]{:S(2)}) async-start(), calls=%async_computation.7 | async-start | bytes 262144 | tf_op jit(solution)/shard_map/pmin | solution.py:42
  407.4 43.7 %all-reduce.41.cloned.1.call-start = ((), (), s32[]{:S(2)}) async-start(), calls=%async_computation.8 | async-start | bytes 524288 | tf_op jit(solution)/shard_map/pmin | solution.py:40
  416.0 138.4 %all-reduce.43.cloned.1.call-start = ((), (), s32[]{:S(2)}) async-start(), calls=%async_computation.9 | async-start | bytes 131072 | tf_op jit(solution)/shard_map/pmin | solution.py:38
  511.5 65.8 %all-reduce.45.cloned.1.call-start = ((), (), s32[]{:S(2)}) async-start(), calls=%async_computation.10 | async-start | bytes 262144 | tf_op jit(solution)/shard_map/pmin | solution.py:42
  561.5 43.6 %all-reduce.47.cloned.1.call-start = ((), (), s32[]{:S(2)}) async-start(), calls=%async_computation.11 | async-start | bytes 524288 | tf_op jit(solution)/shard_map/pmin | solution.py:40
  570.3 138.1 %all-reduce.49.cloned.1.call-start = ((), (), s32[]{:S(2)}) async-start(), calls=%async_computation.12 | async-start | bytes 131072 | tf_op jit(solution)/shard_map/pmin | solution.py:38
  665.5 65.8 %all-reduce.51.cloned.1.call-start = ((), (), s32[]{:S(2)}) async-start(), calls=%async_computation.13 | async-start | bytes 262144 | tf_op jit(solution)/shard_map/pmin | solution.py:42
  715.5 43.6 %all-reduce.53.cloned.1.call-start = ((), (), s32[]{:S(2)}) async-start(), calls=%async_computation.14 | async-start | bytes 524288 | tf_op jit(solution)/shard_map/pmin | solution.py:40
  724.1 138.3 %all-reduce.55.cloned.1.call-start = ((), (), s32[]{:S(2)}) async-start(), calls=%async_computation.15 | async-start | bytes 131072 | tf_op jit(solution)/shard_map/pmin | solution.py:38
  819.4 65.8 %all-reduce.57.cloned.1.call-start = ((), (), s32[]{:S(2)}) async-start(), calls=%async_computation.16 | async-start | bytes 262144 | tf_op jit(solution)/shard_map/pmin | solution.py:42
  869.5 43.6 %all-reduce.59.cloned.1.call-start = ((), (), s32[]{:S(2)}) async-start(), calls=%async_computation.17 | async-start | bytes 524288 | tf_op jit(solution)/shard_map/pmin | solution.py:40
  878.1 138.3 %all-reduce.61.cloned.1.call-start = ((), (), s32[]{:S(2)}) async-start(), calls=%async_computation.18 | async-start | bytes 131072 | tf_op jit(solution)/shard_map/pmin | solution.py:38
  973.4 65.8 %all-reduce.63.cloned.1.call-start = ((), (), s32[]{:S(2)}) async-start(), calls=%async_computation.19 | async-start | bytes 262144 | tf_op jit(solution)/shard_map/pmin | solution.py:42
  1023.5 43.7 %all-reduce.65.cloned.1.call-start = ((), (), s32[]{:S(2)}) async-start(), calls=%async_computation.20 | async-start | bytes 524288 | tf_op jit(solution)/shard_map/pmin | solution.py:40
  1032.1 138.4 %all-reduce.67.cloned.1.call-start = ((), (), s32[]{:S(2)}) async-start(), calls=%async_computation.21 | async-start | bytes 131072 | tf_op jit(solution)/shard_map/pmin | solution.py:38
  1127.6 65.8 %all-reduce.69.cloned.1.call-start = ((), (), s32[]{:S(2)}) async-start(), calls=%async_computation.22 | async-start | bytes 262144 | tf_op jit(solution)/shard_map/pmin | solution.py:42
  1177.6 43.6 %all-reduce.71.cloned.1.call-start = ((), (), s32[]{:S(2)}) async-start(), calls=%async_computation.23 | async-start | bytes 524288 | tf_op jit(solution)/shard_map/pmin | solution.py:40
  (11 other events, 151.8 us)
Sparse Core Ops, SparseCore 0:
  46.8 43.0 all-reduce.24
  99.4 25.3 all-reduce.28
  127.1 17.0 all-reduce.26
  204.6 41.6 all-reduce.30
  253.5 15.6 all-reduce.32
  271.4 25.5 all-reduce.34
  357.5 42.7 all-reduce.36
  407.5 15.6 all-reduce.38
  425.5 25.5 all-reduce.40
  511.6 42.7 all-reduce.42
  561.7 15.6 all-reduce.44
  579.5 25.5 all-reduce.46
  665.6 42.7 all-reduce.48
  715.6 15.6 all-reduce.50
  733.5 25.5 all-reduce.52
  819.6 42.7 all-reduce.54
  869.6 15.6 all-reduce.56
  887.5 25.5 all-reduce.58
  973.6 42.7 all-reduce.60
  1023.6 15.6 all-reduce.62
  1041.6 25.5 all-reduce.64
  1127.7 42.7 all-reduce.66
  1177.8 15.6 all-reduce.68
  1195.6 25.5 all-reduce.70
where the time goes:
time: 1250 us
  waiting for transfers between devices  625 us (50%)
  other arithmetic  383 us (31%)
  local copies, waits for them, and re-layouts  191 us (15%)
  loops' own time  35.6 us (3%)
  between operations  14.4 us (1%)
    pmin x8, waiting for transfers between devices, local_run(): lax.pmin(jnp.where(in_row & in_col, diag_blk, jnp.inf), ('row', 'sub', 'c...  342 us
    reduce_min x24, other arithmetic, min_plus(): jnp.min(jnp.expand_dims(left_mat, -1) + jnp.expand_dims(right_mat, -3), a...  281 us
    pmin x8, waiting for transfers between devices, local_run(): row_pan = lax.pmin(jnp.where(in_row, row_pan, jnp.inf), ('row', 'sub'))  214 us
    dynamic_slice x1024, local copies, waits for them, and re-layouts, pivot_step(): col_vec = lax.dynamic_slice_in_dim(current, pivot_idx, 1, axis=last_axis)  177 us
    min x1024, other arithmetic, pivot_step(): return jnp.minimum(current, col_vec + row_vec)  84.1 us
    pmin x8, waiting for transfers between devices, local_run(): col_pan = lax.pmin(jnp.where(in_col, col_pan, jnp.inf), 'col')  68.9 us
    another operation x8, loops' own time, close_block(): return lax.fori_loop(0, block_in.shape[-1], pivot_step, block_in)  35.6 us
  transfers between devices with their start and end apart: 24, of which 24 were waited for; matrix products, arithmetic and copies ran while one was open for 5% of the time, Pallas kernels for 0%

commit v1 on v0

v1 whole, which is shorter than its diff:
```python
import functools

import jax
import jax.numpy as jnp
from jax import lax
from jax.experimental import pallas as pl
from jax.experimental.pallas import tpu as pltpu
from jax.sharding import PartitionSpec as P

MESH = pl.DeviceIdType.MESH
BLK = 128
ROUNDS = 8
ROW_PEERS = ((0, 1), (1, 1), (1, 0))
ALL_PEERS = ((1, 0, 1), (1, 1, 1), (0, 0, 1), (0, 1, 1), (1, 0, 0), (0, 1, 0), (1, 1, 0))


def lanes(tiles, idx):
    flat = tiles.reshape(-1, 128)
    idx = jnp.broadcast_to(idx[None], (flat.shape[0] // 8, 8, 128)).reshape(-1, 128)
    return jnp.take_along_axis(flat, idx, axis=1, mode='promise_in_bounds').reshape(tiles.shape)


def kernel(in_ref, out_ref, mat, rowp, colp, dst, cb, brep, brepd, cpr,
           row_send, row_recv, col_send, col_recv, dia_send, dia_recv):
    row, sub, col = lax.axis_index('row'), lax.axis_index('sub'), lax.axis_index('col')
    my_row = row * 2 + sub
    lane = lax.broadcasted_iota(jnp.int32, (8, 128), 1)
    in_grp = lane & 15
    grp_base = lane - in_grp

    def peer(d_col, d_row, d_sub):
        return {'col': (col + d_col) % 2, 'row': (row + d_row) % 2, 'sub': (sub + d_sub) % 2}

    barrier = pltpu.get_barrier_semaphore()
    for offs in ALL_PEERS:
        pl.semaphore_signal(barrier, inc=1, device_id=peer(*offs), device_id_type=MESH)

    def swap_chunks(tiles):
        for bit in (1, 2, 4):
            mask = (lane & (16 * bit)) == 0
            pairs = tiles.reshape(8 // (2 * bit), 2, bit, 8, 128)
            lo, hi = pairs[:, 0].reshape(-1, 128), pairs[:, 1].reshape(-1, 128)
            lo_up = pltpu.roll(lo, 128 - 16 * bit, 1)
            hi_up = pltpu.roll(hi, 16 * bit, 1)
            lo, hi, lo_up, hi_up = (v.reshape(8 // (2 * bit), bit, 8, 128) for v in (lo, hi, lo_up, hi_up))
            tiles = jnp.stack([jnp.where(mask, lo, hi_up), jnp.where(mask, lo_up, hi)], axis=1).reshape(8, 8, 128)
        return tiles

    def row_copy(rnd, x, i):
        d_row, d_sub = ROW_PEERS[i]
        return pltpu.make_async_remote_copy(
            src_ref=rowp.at[rnd, x], dst_ref=rowp.at[rnd, x],
            send_sem=row_send.at[rnd, x, i], recv_sem=row_recv.at[rnd, x],
            device_id=peer(0, d_row, d_sub), device_id_type=MESH)

    def col_copy(rnd, a):
        return pltpu.make_async_remote_copy(
            src_ref=colp.at[rnd, a], dst_ref=colp.at[rnd, a],
            send_sem=col_send.at[rnd, a], recv_sem=col_recv.at[rnd, a],
            device_id=peer(1, 0, 0), device_id_type=MESH)

    def dia_copy(rnd, i):
        return pltpu.make_async_remote_copy(
            src_ref=dst.at[rnd], dst_ref=dst.at[rnd],
            send_sem=dia_send.at[rnd, i], recv_sem=dia_recv.at[rnd],
            device_id=peer(*ALL_PEERS[i]), device_id_type=MESH)

    def send_row(rnd, x):
        for i in range(3):
            row_copy(rnd, x, i).start()

    def send_dia(rnd):
        for i in range(7):
            dia_copy(rnd, i).start()

    def close(rnd, x):
        dst[rnd] = rowp[rnd, x]

        def group(g, carry):
            rg, q = g // 8, g % 8
            cg, half = g // 2, (g % 2) * 8
            pivot_tile = dst[rnd, rg, cg]
            ucol = [lanes(pivot_tile, jnp.full((8, 128), 16 * q + half + p, jnp.int32)) for p in range(8)]
            rows = lanes(dst[rnd, rg], in_grp + 16 * q)
            left = [lanes(dst[rnd, :, cg], grp_base + (half + p)) for p in range(8)]
            for p in range(8):
                for j in range(p + 1, 8):
                    ucol[j] = jnp.minimum(ucol[j], ucol[p] + ucol[j][p:p + 1, :])
                rows = jnp.minimum(rows, ucol[p][None] + rows[:, p:p + 1, :])
            acc = dst[rnd]
            for p in range(8):
                acc = jnp.minimum(acc, left[p][:, None] + rows[:, p:p + 1, :][None])
            dst[rnd] = acc
            return carry
        lax.fori_loop(0, 16, group, 0)

    def make_brep(src, out):
        def one(i, carry):
            out[i] = lanes(src[i // 8], in_grp + 16 * (i % 8))
            return carry
        lax.fori_loop(0, 16, one, 0, unroll=True)

    def product(acc, left, right):
        def pivot(k, acc):
            return jnp.minimum(acc, left(k)[:, None] + right[k // 8, :, pl.ds(k % 8, 1), :][None])
        return lax.fori_loop(0, BLK, pivot, acc, unroll=True)

    def close_and_send(rnd, x):
        close(rnd, x)
        send_dia(rnd)

    slot_r = jnp.where(my_row == 0, 0, ROUNDS)
    slot_c = jnp.where(col == 0, 0, ROUNDS)
    for a in range(2):
        for x in range(4):
            for r in range(2):
                tiles = swap_chunks(in_ref[a, 64 * r:64 * r + 64, BLK * x:BLK * x + BLK].reshape(8, 8, 128))
                mat[a, x, r] = tiles
                if a == 0:
                    rowp[slot_r, x, r] = tiles
                if x == 0:
                    colp[slot_c, a, r] = tiles

    pl.semaphore_wait(barrier, 7)

    @pl.when((my_row == 0) & (col == 0))
    def _():
        close_and_send(0, 0)

    @pl.when(my_row == 0)
    def _():
        for x in range(4):
            send_row(0, x)

    @pl.when(col == 0)
    def _():
        for a in range(2):
            col_copy(0, a).start()

    def one_round(k, carry):
        n = k + 1
        more = n < ROUNDS
        own_row = (my_row == n % 4) & more
        own_col = (col == n % 2) & more
        a1 = jnp.minimum(n // 4, 1)
        x1 = jnp.minimum((n + jnp.where(col == n % 2, 0, 1)) // 2, 3)

        @pl.when((my_row != k % 4) | (col != k % 2))
        def _():
            dia_copy(k, 0).wait_recv()

        def wait_row(x):
            @pl.when(my_row != k % 4)
            def _():
                row_copy(k, x, 0).wait_recv()

        make_brep(dst.at[k], brepd)
        wait_row(x1)
        make_brep(rowp.at[k, x1], brep.at[x1])

        def head(h, carry):
            a = jnp.where(h == 0, a1, 1 - a1)

            @pl.when(col != k % 2)
            def _():
                col_copy(k, a).wait_recv()

            pan = colp.at[k, a]
            cpr[...] = product(pan[...], lambda p: lanes(pan[:, p // 16], grp_base + p % 16), brepd)
            tab = cb.at[a]

            def fly(p):
                avs = lanes(cpr[:, p // 16], grp_base + p % 16)
                tab[p] = avs
                return avs
            acc = product(mat[a, x1], fly, brep.at[x1])
            mat[a, x1] = acc
            send_it = own_row & (h == 0)
            rowp[jnp.where(send_it, n, ROUNDS), x1] = acc
            colp[jnp.where(own_col, n, ROUNDS), a] = acc

            @pl.when(send_it)
            def _():
                send_row(n, x1)

            @pl.when(own_col)
            def _():
                col_copy(n, a).start()

            @pl.when(send_it & own_col)
            def _():
                close_and_send(n, x1)
            return carry
        lax.fori_loop(0, 2, head, 0)

        def tail(t, carry):
            h = t // 3
            a = jnp.where(h == 0, a1, 1 - a1)
            x = (x1 + 1 + t % 3) % 4

            @pl.when(h == 0)
            def _():
                wait_row(x)
                make_brep(rowp.at[k, x], brep.at[x])

            tab = cb.at[a]
            acc = product(mat[a, x], lambda p: tab[p], brep.at[x])
            mat[a, x] = acc
            send_it = own_row & (h == 0)
            rowp[jnp.where(send_it, n, ROUNDS), x] = acc

            @pl.when(send_it)
            def _():
                send_row(n, x)
            return carry
        lax.fori_loop(0, 6, tail, 0)
        return carry
    lax.fori_loop(0, ROUNDS, one_round, 0)

    for a in range(2):
        for x in range(4):
            for r in range(2):
                tiles = swap_chunks(mat[a, x, r])
                out_ref[a, 64 * r:64 * r + 64, BLK * x:BLK * x + BLK] = tiles.reshape(64, 128)

    def drain(k, carry):
        @pl.when(my_row == k % 4)
        def _():
            for x in range(4):
                for i in range(3):
                    row_copy(k, x, i).wait_send()

        @pl.when(col == k % 2)
        def _():
            for a in range(2):
                col_copy(k, a).wait_send()

        @pl.when((my_row == k % 4) & (col == k % 2))
        def _():
            for i in range(7):
                dia_copy(k, i).wait_send()
        return carry
    lax.fori_loop(0, ROUNDS, drain, 0)


def solution(mesh):
    spec = P(('parts', 'row', 'sub'), None, 'col')
    tile = (8, 128)
    dma = pltpu.SemaphoreType.DMA

    def local_run(local_dist):
        return pl.pallas_call(
            kernel,
            out_shape=jax.ShapeDtypeStruct(local_dist.shape, local_dist.dtype),
            in_specs=[pl.BlockSpec(memory_space=pltpu.VMEM)],
            out_specs=pl.BlockSpec(memory_space=pltpu.VMEM),
            scratch_shapes=[
                pltpu.VMEM((2, 4, 2, 8) + tile, jnp.float32),
                pltpu.VMEM((ROUNDS + 1, 4, 2, 8) + tile, jnp.float32),
                pltpu.VMEM((ROUNDS + 1, 2, 2, 8) + tile, jnp.float32),
                pltpu.VMEM((ROUNDS, 2, 8) + tile, jnp.float32),
                pltpu.VMEM((2, BLK, 2) + tile, jnp.float32),
                pltpu.VMEM((4, 16, 8) + tile, jnp.float32),
                pltpu.VMEM((16, 8) + tile, jnp.float32),
                pltpu.VMEM((2, 8) + tile, jnp.float32),
                dma((ROUNDS, 4, 3)), dma((ROUNDS, 4)),
                dma((ROUNDS, 2)), dma((ROUNDS, 2)),
                dma((ROUNDS, 7)), dma((ROUNDS,)),
            ],
            compiler_params=pltpu.CompilerParams(collective_id=0, has_side_effects=True),
            name='apsp',
        )(local_dist)

    return jax.shard_map(local_run, mesh=mesh, in_specs=(spec,), out_specs=spec, check_vma=False)
```

time: 1250 us -> 107 us (0.09)
  the two profiles are of different devices: /device:TPU:1 before, /device:TPU:0 now
where the time goes in v1:
time: 107 us
  Pallas kernels  105 us (98%)
  local copies, waits for them, and re-layouts  1.87 us (2%)
    pallas_call x1, Pallas kernels, local_run(): pl.pallas_call(kernel, out_shape=jax.ShapeDtypeStruct(local_dist.shape, l...  105 us

profile of v1, /device:TPU:0, one launch (start us, length us, event | category | flops | bytes accessed | tf_op | source)
XLA Modules:
  0.0 107.3 jit_solution(18076512313404558053)
XLA Ops:
  0.0 105.4 %apsp.1 = f32[2,128,512]{2,1,0:T(8,128)} custom-call(f32[2,128,512]{2,1,0:T(8,128)} %in_ref.1), custom_call_target="tpu_custom_call" | custom-call | tf_op jit(solution)/shard_map/apsp/pallas_call | solution.py:252
  105.4 1.9 %copy.3 = f32[2,128,512]{2,1,0:T(8,128)} copy(f32[2,128,512]{2,1,0:T(8,128)} %apsp.1) | data formatting | bytes 1048576

commit v2 on v1

--- a/solution.py
+++ b/solution.py
@@ -21,7 +21,8 @@
 
 
 def kernel(in_ref, out_ref, mat, rowp, colp, dst, cb, brep, brepd, cpr,
-           row_send, row_recv, col_send, col_recv, dia_send, dia_recv):
+
+           row_send, row_recv, col_send, col_recv, dia_send, dia_fwd, dia_recv):
     row, sub, col = lax.axis_index('row'), lax.axis_index('sub'), lax.axis_index('col')
     my_row = row * 2 + sub
     lane = lax.broadcasted_iota(jnp.int32, (8, 128), 1)
@@ -60,21 +61,32 @@
             device_id=peer(1, 0, 0), device_id_type=MESH)
 
     def dia_copy(rnd, i):
+        turn = rnd % 2
+        offs = ((1, turn, 1), (1, 1 - turn, 1), (0, 1, 1), (0, 0, 1))[i]
         return pltpu.make_async_remote_copy(
             src_ref=dst.at[rnd], dst_ref=dst.at[rnd],
             send_sem=dia_send.at[rnd, i], recv_sem=dia_recv.at[rnd],
-            device_id=peer(*ALL_PEERS[i]), device_id_type=MESH)
+            device_id=peer(*offs), device_id_type=MESH)
+
+    def dia_pass(rnd):
+        return pltpu.make_async_remote_copy(
+            src_ref=dst.at[rnd], dst_ref=dst.at[rnd],
+            send_sem=dia_fwd.at[rnd], recv_sem=dia_recv.at[rnd],
+            device_id=peer(0, 0, 1), device_id_type=MESH)
+
+    def passes(rnd):
+        return (sub != rnd % 2) & ((col != rnd % 2) | (row != (rnd % 4) // 2))
 
     def send_row(rnd, x):
         for i in range(3):
             row_copy(rnd, x, i).start()
 
     def send_dia(rnd):
-        for i in range(7):
+        for i in range(4):
             dia_copy(rnd, i).start()
 
-    def close(rnd, x):
-        dst[rnd] = rowp[rnd, x]
+    def close(rnd, a, x):
+        dst[rnd] = mat[a, x]
 
         def group(g, carry):
             rg, q = g // 8, g % 8
@@ -105,8 +117,8 @@
             return jnp.minimum(acc, left(k)[:, None] + right[k // 8, :, pl.ds(k % 8, 1), :][None])
         return lax.fori_loop(0, BLK, pivot, acc, unroll=True)
 
-    def close_and_send(rnd, x):
-        close(rnd, x)
+    def close_and_send(rnd, a, x):
+        close(rnd, a, x)
         send_dia(rnd)
 
     slot_r = jnp.where(my_row == 0, 0, ROUNDS)
@@ -125,17 +137,24 @@
 
     @pl.when((my_row == 0) & (col == 0))
     def _():
-        close_and_send(0, 0)
+        close_and_send(0, 0, 0)
 
     @pl.when(my_row == 0)
     def _():
         for x in range(4):
-            send_row(0, x)
+            if x == 0:
+                @pl.when(col != 0)
+                def _():
+                    send_row(0, 0)
+            else:
+                send_row(0, x)
 
     @pl.when(col == 0)
     def _():
-        for a in range(2):
-            col_copy(0, a).start()
+        @pl.when(my_row != 0)
+        def _():
+            col_copy(0, 0).start()
+        col_copy(0, 1).start()
 
     def one_round(k, carry):
         n = k + 1
@@ -143,14 +162,20 @@
         own_row = (my_row == n % 4) & more
         own_col = (col == n % 2) & more
         a1 = jnp.minimum(n // 4, 1)
-        x1 = jnp.minimum((n + jnp.where(col == n % 2, 0, 1)) // 2, 3)
-
-        @pl.when((my_row != k % 4) | (col != k % 2))
+        x1 = ((n + jnp.where(col == n % 2, 0, 1)) // 2) % 4
+        xk = k // 2
+        is_row, is_col = my_row == k % 4, col == k % 2
+
+        @pl.when(~is_row | ~is_col)
         def _():
             dia_copy(k, 0).wait_recv()
 
+        @pl.when(passes(k))
+        def _():
+            dia_pass(k).start()
+
         def wait_row(x):
-            @pl.when(my_row != k % 4)
+            @pl.when(~is_row)
             def _():
                 row_copy(k, x, 0).wait_recv()
 
@@ -161,12 +186,31 @@
         def head(h, carry):
             a = jnp.where(h == 0, a1, 1 - a1)
 
-            @pl.when(col != k % 2)
+            on_diag = is_row & (a == k // 4)
+            send_it = own_row & (h == 0)
+
+            @pl.when(~is_col & ~on_diag)
             def _():
                 col_copy(k, a).wait_recv()
 
-            pan = colp.at[k, a]
-            cpr[...] = product(pan[...], lambda p: lanes(pan[:, p // 16], grp_base + p % 16), brepd)
+            @pl.when(on_diag)
+            def _():
+                cpr[...] = dst[k]
+
+            @pl.when(~on_diag)
+            def _():
+                pan = colp.at[k, a]
+                cpr[...] = product(pan[...], lambda p: lanes(pan[:, p // 16], grp_base + p % 16), brepd)
+
+            @pl.when(is_col)
+            def _():
+                mat[a, xk] = cpr[...]
+
+            @pl.when(is_col & send_it)
+            def _():
+                rowp[n, xk] = cpr[...]
+                send_row(n, xk)
+
             tab = cb.at[a]
 
             def fly(p):
@@ -175,21 +219,20 @@
                 return avs
             acc = product(mat[a, x1], fly, brep.at[x1])
             mat[a, x1] = acc
-            send_it = own_row & (h == 0)
             rowp[jnp.where(send_it, n, ROUNDS), x1] = acc
             colp[jnp.where(own_col, n, ROUNDS), a] = acc
 
-            @pl.when(send_it)
+            @pl.when(send_it & ~own_col)
             def _():
                 send_row(n, x1)
 
-            @pl.when(own_col)
+            @pl.when(own_col & ~send_it)
             def _():
                 col_copy(n, a).start()
 
             @pl.when(send_it & own_col)
             def _():
-                close_and_send(n, x1)
+                close_and_send(n, a, x1)
             return carry
         lax.fori_loop(0, 2, head, 0)
 
@@ -198,20 +241,22 @@
             a = jnp.where(h == 0, a1, 1 - a1)
             x = (x1 + 1 + t % 3) % 4
 
-            @pl.when(h == 0)
-            def _():
-                wait_row(x)
-                make_brep(rowp.at[k, x], brep.at[x])
-
-            tab = cb.at[a]
-            acc = product(mat[a, x], lambda p: tab[p], brep.at[x])
-            mat[a, x] = acc
-            send_it = own_row & (h == 0)
-            rowp[jnp.where(send_it, n, ROUNDS), x] = acc
-
-            @pl.when(send_it)
-            def _():
-                send_row(n, x)
+            @pl.when((col != k % 2) | (t % 3 != 2))
+            def _():
+                @pl.when(h == 0)
+                def _():
+                    wait_row(x)
+                    make_brep(rowp.at[k, x], brep.at[x])
+
+                tab = cb.at[a]
+                acc = product(mat[a, x], lambda p: tab[p], brep.at[x])
+                mat[a, x] = acc
+                send_it = own_row & (h == 0)
+                rowp[jnp.where(send_it, n, ROUNDS), x] = acc
+
+                @pl.when(send_it)
+                def _():
+                    send_row(n, x)
             return carry
         lax.fori_loop(0, 6, tail, 0)
         return carry
@@ -224,21 +269,25 @@
                 out_ref[a, 64 * r:64 * r + 64, BLK * x:BLK * x + BLK] = tiles.reshape(64, 128)
 
     def drain(k, carry):
-        @pl.when(my_row == k % 4)
-        def _():
-            for x in range(4):
+        is_row, is_col = my_row == k % 4, col == k % 2
+        for x in range(4):
+            @pl.when(is_row & (~is_col | (x != k // 2)))
+            def _():
                 for i in range(3):
                     row_copy(k, x, i).wait_send()
-
-        @pl.when(col == k % 2)
-        def _():
-            for a in range(2):
+        for a in range(2):
+            @pl.when(is_col & (~is_row | (a != k // 4)))
+            def _():
                 col_copy(k, a).wait_send()
 
-        @pl.when((my_row == k % 4) & (col == k % 2))
-        def _():
-            for i in range(7):
+        @pl.when(is_row & is_col)
+        def _():
+            for i in range(4):
                 dia_copy(k, i).wait_send()
+
+        @pl.when(passes(k))
+        def _():
+            dia_pass(k).wait_send()
         return carry
     lax.fori_loop(0, ROUNDS, drain, 0)
 
@@ -265,7 +314,7 @@
                 pltpu.VMEM((2, 8) + tile, jnp.float32),
                 dma((ROUNDS, 4, 3)), dma((ROUNDS, 4)),
                 dma((ROUNDS, 2)), dma((ROUNDS, 2)),
-                dma((ROUNDS, 7)), dma((ROUNDS,)),
+                dma((ROUNDS, 4)), dma((ROUNDS,)), dma((ROUNDS,)),
             ],
             compiler_params=pltpu.CompilerParams(collective_id=0, has_side_effects=True),
             name='apsp',

time: 107 us -> 93.4 us (0.87)
  the two profiles are of different devices: /device:TPU:0 before, /device:TPU:1 now
where the time goes in v2:
time: 93.4 us; the launch traced here: 93.2 us
  Pallas kernels  91.3 us (98%)
  local copies, waits for them, and re-layouts  1.87 us (2%)
    pallas_call x1, Pallas kernels, local_run(): pl.pallas_call(kernel, out_shape=jax.ShapeDtypeStruct(local_dist.shape, l...  91.3 us
    unnamed x1, local copies, waits for them, and re-layouts  1.87 us

profile of v2, /device:TPU:1, one launch (start us, length us, event | category | flops | bytes accessed | tf_op | source)
XLA Modules:
  0.0 93.2 jit_solution(4149437701521329650)
XLA Ops:
  0.0 91.3 %apsp.1 = f32[2,128,512]{2,1,0:T(8,128)} custom-call(f32[2,128,512]{2,1,0:T(8,128)} %in_ref.1), custom_call_target="tpu_custom_call" | custom-call | tf_op jit(solution)/shard_map/apsp/pallas_call | solution.py:301
  91.3 1.9 %copy.3 = f32[2,128,512]{2,1,0:T(8,128)} copy(f32[2,128,512]{2,1,0:T(8,128)} %apsp.1) | data formatting | bytes 1048576

commit v3 on v2

--- a/solution.py
+++ b/solution.py
@@ -10,6 +10,7 @@
 MESH = pl.DeviceIdType.MESH
 BLK = 128
 ROUNDS = 8
+HEAD_STEP, TAIL_STEP = 128, 64
 ROW_PEERS = ((0, 1), (1, 1), (1, 0))
 ALL_PEERS = ((1, 0, 1), (1, 1, 1), (0, 0, 1), (0, 1, 1), (1, 0, 0), (0, 1, 0), (1, 1, 0))
 
@@ -112,10 +113,13 @@
             return carry
         lax.fori_loop(0, 16, one, 0, unroll=True)
 
-    def product(acc, left, right):
-        def pivot(k, acc):
-            return jnp.minimum(acc, left(k)[:, None] + right[k // 8, :, pl.ds(k % 8, 1), :][None])
-        return lax.fori_loop(0, BLK, pivot, acc, unroll=True)
+    def product(acc, left, right, step):
+        def chunk(i, acc):
+            def pivot(u, acc):
+                b = right[i * (step // 8) + u // 8, :, pl.ds(u % 8, 1), :]
+                return jnp.minimum(acc, left(i * (step // 16) + u // 16, i * step + u, u % 16)[:, None] + b[None])
+            return lax.fori_loop(0, step, pivot, acc, unroll=True)
+        return lax.fori_loop(0, BLK // step, chunk, acc, unroll=step == BLK)
 
     def close_and_send(rnd, a, x):
         close(rnd, a, x)
@@ -200,7 +204,7 @@
             @pl.when(~on_diag)
             def _():
                 pan = colp.at[k, a]
-                cpr[...] = product(pan[...], lambda p: lanes(pan[:, p // 16], grp_base + p % 16), brepd)
+                cpr[...] = product(pan[...], lambda c, p, l: lanes(pan[:, c], grp_base + l), brepd, HEAD_STEP)
 
             @pl.when(is_col)
             def _():
@@ -213,11 +217,11 @@
 
             tab = cb.at[a]
 
-            def fly(p):
-                avs = lanes(cpr[:, p // 16], grp_base + p % 16)
+            def fly(c, p, l):
+                avs = lanes(cpr[:, c], grp_base + l)
                 tab[p] = avs
                 return avs
-            acc = product(mat[a, x1], fly, brep.at[x1])
+            acc = product(mat[a, x1], fly, brep.at[x1], HEAD_STEP)
             mat[a, x1] = acc
             rowp[jnp.where(send_it, n, ROUNDS), x1] = acc
             colp[jnp.where(own_col, n, ROUNDS), a] = acc
@@ -249,7 +253,7 @@
                     make_brep(rowp.at[k, x], brep.at[x])
 
                 tab = cb.at[a]
-                acc = product(mat[a, x], lambda p: tab[p], brep.at[x])
+                acc = product(mat[a, x], lambda c, p, l: tab[p], brep.at[x], TAIL_STEP)
                 mat[a, x] = acc
                 send_it = own_row & (h == 0)
                 rowp[jnp.where(send_it, n, ROUNDS), x] = acc

time: 93.4 us -> 89.9 us (0.963)
  Pallas kernels: 91.3 us -> 87.8 us
    pallas_call x1, Pallas kernels: 91.3 us -> 87.8 us  [local_run(): pl.pallas_call(kernel, out_shape=jax.ShapeDtypeStruct(local_dist.shape, l...]
where the time goes in v3:
time: 89.9 us; the launch traced here: 89.7 us
  Pallas kernels  87.8 us (98%)
  local copies, waits for them, and re-layouts  1.87 us (2%)
    pallas_call x1, Pallas kernels, local_run(): pl.pallas_call(kernel, out_shape=jax.ShapeDtypeStruct(local_dist.shape, l...  87.8 us
    unnamed x1, local copies, waits for them, and re-layouts  1.87 us

profile of v3, /device:TPU:1, one launch (start us, length us, event | category | flops | bytes accessed | tf_op | source)
XLA Modules:
  0.0 89.7 jit_solution(16917698246351405776)
XLA Ops:
  0.0 87.8 %apsp.1 = f32[2,128,512]{2,1,0:T(8,128)} custom-call(f32[2,128,512]{2,1,0:T(8,128)} %in_ref.1), custom_call_target="tpu_custom_call" | custom-call | tf_op jit(solution)/shard_map/apsp/pallas_call | solution.py:305
  87.8 1.9 %copy.3 = f32[2,128,512]{2,1,0:T(8,128)} copy(f32[2,128,512]{2,1,0:T(8,128)} %apsp.1) | data formatting | bytes 1048576

commit v4 on v3

--- a/solution.py
+++ b/solution.py
@@ -10,7 +10,7 @@
 MESH = pl.DeviceIdType.MESH
 BLK = 128
 ROUNDS = 8
-HEAD_STEP, TAIL_STEP = 128, 64
+HEAD_STEP, TAIL_STEP = 64, 64
 ROW_PEERS = ((0, 1), (1, 1), (1, 0))
 ALL_PEERS = ((1, 0, 1), (1, 1, 1), (0, 0, 1), (0, 1, 1), (1, 0, 0), (0, 1, 0), (1, 1, 0))
 

time: 89.9 us -> 90.8 us (1.010)
  no operation moved by 1% of the time
where the time goes in v4:
time: 90.8 us; the launch traced here: 90.6 us
  Pallas kernels  88.7 us (98%)
  local copies, waits for them, and re-layouts  1.87 us (2%)
    pallas_call x1, Pallas kernels, local_run(): pl.pallas_call(kernel, out_shape=jax.ShapeDtypeStruct(local_dist.shape, l...  88.7 us
    unnamed x1, local copies, waits for them, and re-layouts  1.87 us

profile of v4, /device:TPU:1, one launch (start us, length us, event | category | flops | bytes accessed | tf_op | source)
XLA Modules:
  0.0 90.6 jit_solution(15642020352041216254)
XLA Ops:
  0.0 88.7 %apsp.1 = f32[2,128,512]{2,1,0:T(8,128)} custom-call(f32[2,128,512]{2,1,0:T(8,128)} %in_ref.1), custom_call_target="tpu_custom_call" | custom-call | tf_op jit(solution)/shard_map/apsp/pallas_call | solution.py:305
  88.7 1.9 %copy.3 = f32[2,128,512]{2,1,0:T(8,128)} copy(f32[2,128,512]{2,1,0:T(8,128)} %apsp.1) | data formatting | bytes 1048576

commit v5 on v3

--- a/solution.py
+++ b/solution.py
@@ -17,7 +17,7 @@
 
 def lanes(tiles, idx):
     flat = tiles.reshape(-1, 128)
-    idx = jnp.broadcast_to(idx[None], (flat.shape[0] // 8, 8, 128)).reshape(-1, 128)
+    idx = jnp.broadcast_to(idx, tiles.shape).reshape(-1, 128)
     return jnp.take_along_axis(flat, idx, axis=1, mode='promise_in_bounds').reshape(tiles.shape)
 
 
@@ -29,6 +29,7 @@
     lane = lax.broadcasted_iota(jnp.int32, (8, 128), 1)
     in_grp = lane & 15
     grp_base = lane - in_grp
+    nth_pivot = lax.broadcasted_iota(jnp.int32, (8, 8, 128), 0)
 
     def peer(d_col, d_row, d_sub):
         return {'col': (col + d_col) % 2, 'row': (row + d_row) % 2, 'sub': (sub + d_sub) % 2}
@@ -90,34 +91,37 @@
         dst[rnd] = mat[a, x]
 
         def group(g, carry):
-            rg, q = g // 8, g % 8
-            cg, half = g // 2, (g % 2) * 8
-            pivot_tile = dst[rnd, rg, cg]
-            ucol = [lanes(pivot_tile, jnp.full((8, 128), 16 * q + half + p, jnp.int32)) for p in range(8)]
-            rows = lanes(dst[rnd, rg], in_grp + 16 * q)
-            left = [lanes(dst[rnd, :, cg], grp_base + (half + p)) for p in range(8)]
+            rg, cg = lax.div(g, 8), lax.div(g, 2)
+            q, half = lax.rem(g, 8), lax.rem(g, 2) * 8
+            ucol = lanes(jnp.broadcast_to(dst[rnd, rg, cg][None], (8, 8, 128)), nth_pivot + (16 * q + half))
+            rows = lanes(dst[rnd, rg], in_grp[None] + 16 * q)
+            left = lanes(jnp.broadcast_to(dst[rnd, :, cg][None], (8, 2, 8, 128)),
+                         (nth_pivot + (grp_base + half)[None])[:, None])
             for p in range(8):
-                for j in range(p + 1, 8):
-                    ucol[j] = jnp.minimum(ucol[j], ucol[p] + ucol[j][p:p + 1, :])
-                rows = jnp.minimum(rows, ucol[p][None] + rows[:, p:p + 1, :])
-            acc = dst[rnd]
+                rows = jnp.minimum(rows, ucol[0][None] + rows[:, p:p + 1, :])
+                if p < 7:
+                    ucol = jnp.minimum(ucol[1:], ucol[0][None] + ucol[1:, p:p + 1, :])
+            block = dst[rnd]
             for p in range(8):
-                acc = jnp.minimum(acc, left[p][:, None] + rows[:, p:p + 1, :][None])
-            dst[rnd] = acc
+                block = jnp.minimum(block, left[p][:, None] + rows[:, p:p + 1, :][None])
+            dst[rnd] = block
             return carry
-        lax.fori_loop(0, 16, group, 0)
+
+        def groups(i, carry):
+            return lax.fori_loop(0, 4, lambda u, c: group(i * 4 + u, c), carry, unroll=True)
+        lax.fori_loop(0, 4, groups, 0)
 
     def make_brep(src, out):
         def one(i, carry):
-            out[i] = lanes(src[i // 8], in_grp + 16 * (i % 8))
+            out[i] = lanes(src[lax.div(i, 8)], in_grp + 16 * lax.rem(i, 8))
             return carry
         lax.fori_loop(0, 16, one, 0, unroll=True)
 
     def product(acc, left, right, step):
         def chunk(i, acc):
             def pivot(u, acc):
-                b = right[i * (step // 8) + u // 8, :, pl.ds(u % 8, 1), :]
-                return jnp.minimum(acc, left(i * (step // 16) + u // 16, i * step + u, u % 16)[:, None] + b[None])
+                b = right[i * (step // 8) + lax.div(u, 8), :, pl.ds(lax.rem(u, 8), 1), :]
+                return jnp.minimum(acc, left(i * (step // 16) + lax.div(u, 16), i * step + u, lax.rem(u, 16))[:, None] + b[None])
             return lax.fori_loop(0, step, pivot, acc, unroll=True)
         return lax.fori_loop(0, BLK // step, chunk, acc, unroll=step == BLK)
 

time: 89.9 us -> 89.7 us (level)
  no operation moved by 1% of the time
where the time goes in v5:
time: 89.7 us; the launch traced here: 89.5 us
  Pallas kernels  87.6 us (98%)
  local copies, waits for them, and re-layouts  1.87 us (2%)
    pallas_call x1, Pallas kernels, local_run(): pl.pallas_call(kernel, out_shape=jax.ShapeDtypeStruct(local_dist.shape, l...  87.6 us
    unnamed x1, local copies, waits for them, and re-layouts  1.87 us

profile of v5, /device:TPU:1, one launch (start us, length us, event | category | flops | bytes accessed | tf_op | source)
XLA Modules:
  0.0 89.5 jit_solution(9800874906440340860)
XLA Ops:
  0.0 87.6 %apsp.1 = f32[2,128,512]{2,1,0:T(8,128)} custom-call(f32[2,128,512]{2,1,0:T(8,128)} %in_ref.1), custom_call_target="tpu_custom_call" | custom-call | tf_op jit(solution)/shard_map/apsp/pallas_call | solution.py:309
  87.6 1.9 %copy.3 = f32[2,128,512]{2,1,0:T(8,128)} copy(f32[2,128,512]{2,1,0:T(8,128)} %apsp.1) | data formatting | bytes 1048576

commit v6 on v5

--- a/solution.py
+++ b/solution.py
@@ -10,7 +10,6 @@
 MESH = pl.DeviceIdType.MESH
 BLK = 128
 ROUNDS = 8
-HEAD_STEP, TAIL_STEP = 128, 64
 ROW_PEERS = ((0, 1), (1, 1), (1, 0))
 ALL_PEERS = ((1, 0, 1), (1, 1, 1), (0, 0, 1), (0, 1, 1), (1, 0, 0), (0, 1, 0), (1, 1, 0))
 
@@ -111,19 +110,36 @@
             return lax.fori_loop(0, 4, lambda u, c: group(i * 4 + u, c), carry, unroll=True)
         lax.fori_loop(0, 4, groups, 0)
 
-    def make_brep(src, out):
-        def one(i, carry):
-            out[i] = lanes(src[lax.div(i, 8)], in_grp + 16 * lax.rem(i, 8))
-            return carry
-        lax.fori_loop(0, 16, one, 0, unroll=True)
-
-    def product(acc, left, right, step):
+    def spread(src, out):
+        def build(g):
+            out[g] = lanes(src[lax.div(g, 8)], (in_grp + 16 * lax.rem(g, 8))[None])
+        return build
+
+    def product(acc, left, right, step, build=None):
         def chunk(i, acc):
-            def pivot(u, acc):
-                b = right[i * (step // 8) + lax.div(u, 8), :, pl.ds(lax.rem(u, 8), 1), :]
-                return jnp.minimum(acc, left(i * (step // 16) + lax.div(u, 16), i * step + u, lax.rem(u, 16))[:, None] + b[None])
-            return lax.fori_loop(0, step, pivot, acc, unroll=True)
-        return lax.fori_loop(0, BLK // step, chunk, acc, unroll=step == BLK)
+            def group(u, acc):
+                g = i * step + u
+                if build is not None:
+                    build(g)
+                for s in range(8):
+                    acc = jnp.minimum(acc, left(g, s)[:, None] + right[g, :, s:s + 1, :][None])
+                return acc
+            return lax.fori_loop(0, step, group, acc, unroll=True)
+        if step == 16:
+            return chunk(0, acc)
+        return lax.fori_loop(0, 16 // step, chunk, acc)
+
+    def from_panel(ref):
+        def left(g, s):
+            return lanes(ref(lax.div(g, 2)), grp_base + (lax.rem(g, 2) * 8 + s))
+        return left
+
+    def saving(left, save):
+        def both(g, s):
+            cols = left(g, s)
+            save(8 * g + s, cols)
+            return cols
+        return both
 
     def close_and_send(rnd, a, x):
         close(rnd, a, x)
@@ -187,62 +203,72 @@
             def _():
                 row_copy(k, x, 0).wait_recv()
 
-        make_brep(dst.at[k], brepd)
-        wait_row(x1)
-        make_brep(rowp.at[k, x1], brep.at[x1])
+        spread_dia = spread(dst.at[k], brepd)
+
+        def spread_row(x):
+            return spread(rowp.at[k, x], brep.at[x])
+
+        def wait_col(a):
+            @pl.when((col != k % 2) & ((my_row != k % 4) | (a != k // 4)))
+            def _():
+                col_copy(k, a).wait_recv()
+
+        def one_panel(a, build):
+            pan = colp.at[k, a]
+            cpr[a] = product(pan[...], from_panel(lambda c: pan[:, c]), brepd, 8, build)
 
         def head(h, carry):
             a = jnp.where(h == 0, a1, 1 - a1)
-
-            on_diag = is_row & (a == k // 4)
-            send_it = own_row & (h == 0)
-
-            @pl.when(~is_col & ~on_diag)
-            def _():
-                col_copy(k, a).wait_recv()
-
-            @pl.when(on_diag)
-            def _():
-                cpr[...] = dst[k]
-
-            @pl.when(~on_diag)
-            def _():
-                pan = colp.at[k, a]
-                cpr[...] = product(pan[...], lambda c, p, l: lanes(pan[:, c], grp_base + l), brepd, HEAD_STEP)
+            wait_col(a)
+
+            @pl.when(h == 0)
+            def _():
+                one_panel(a, spread_dia)
+
+            @pl.when(h == 1)
+            def _():
+                one_panel(a, None)
 
             @pl.when(is_col)
             def _():
-                mat[a, xk] = cpr[...]
-
-            @pl.when(is_col & send_it)
-            def _():
-                rowp[n, xk] = cpr[...]
+                mat[a, xk] = cpr[a]
+
+            @pl.when(is_col & (h == 0))
+            def _():
+                rowp[n, xk] = cpr[a]
                 send_row(n, xk)
 
-            tab = cb.at[a]
-
-            def fly(c, p, l):
-                avs = lanes(cpr[:, c], grp_base + l)
-                tab[p] = avs
-                return avs
-            acc = product(mat[a, x1], fly, brep.at[x1], HEAD_STEP)
-            mat[a, x1] = acc
-            rowp[jnp.where(send_it, n, ROUNDS), x1] = acc
-            colp[jnp.where(own_col, n, ROUNDS), a] = acc
-
-            @pl.when(send_it & ~own_col)
-            def _():
+            tab = cb.at[:, a]
+
+            def keep(p, cols):
+                tab[p] = cols
+
+            def fly(build):
+                mat[a, x1] = product(mat[a, x1], saving(from_panel(lambda c: cpr[a, :, c]), keep), brep.at[x1], 8, build)
+
+            @pl.when(h == 0)
+            def _():
+                wait_row(x1)
+                fly(spread_row(x1))
+
+            @pl.when(h == 1)
+            def _():
+                fly(None)
+
+            @pl.when((h == 0) & (col != n % 2))
+            def _():
+                rowp[n, x1] = mat[a, x1]
                 send_row(n, x1)
 
-            @pl.when(own_col & ~send_it)
-            def _():
+            @pl.when((h == 1) & (col == n % 2))
+            def _():
+                colp[n, a] = mat[a, x1]
                 col_copy(n, a).start()
 
-            @pl.when(send_it & own_col)
+            @pl.when((h == 0) & (col == n % 2))
             def _():
                 close_and_send(n, a, x1)
             return carry
-        lax.fori_loop(0, 2, head, 0)
 
         def tail(t, carry):
             h = t // 3
@@ -251,22 +277,74 @@
 
             @pl.when((col != k % 2) | (t % 3 != 2))
             def _():
+                tab = cb.at[:, a]
+
                 @pl.when(h == 0)
                 def _():
                     wait_row(x)
-                    make_brep(rowp.at[k, x], brep.at[x])
-
-                tab = cb.at[a]
-                acc = product(mat[a, x], lambda c, p, l: tab[p], brep.at[x], TAIL_STEP)
-                mat[a, x] = acc
-                send_it = own_row & (h == 0)
-                rowp[jnp.where(send_it, n, ROUNDS), x] = acc
-
-                @pl.when(send_it)
+                    acc = product(mat[a, x], lambda g, s: tab[8 * g + s], brep.at[x], 8, spread_row(x))
+                    mat[a, x] = acc
+                    rowp[n, x] = acc
+                    send_row(n, x)
+
+                @pl.when(h == 1)
                 def _():
-                    send_row(n, x)
+                    mat[a, x] = product(mat[a, x], lambda g, s: tab[8 * g + s], brep.at[x], 8)
             return carry
-        lax.fori_loop(0, 6, tail, 0)
+
+        @pl.when(own_row)
+        def _():
+            lax.fori_loop(0, 2, head, 0)
+            lax.fori_loop(0, 6, tail, 0)
+
+        def four(tiles):
+            return tiles.reshape((4,) + tiles.shape[2:])
+
+        def two(tiles):
+            return tiles.reshape((2, 2) + tiles.shape[1:])
+
+        @pl.when(~own_row)
+        def _():
+            @pl.when(is_row)
+            def _():
+                wait_col(1 - k // 4)
+                one_panel(1 - k // 4, spread_dia)
+                cpr[k // 4] = dst[k]
+
+            @pl.when(~is_row)
+            def _():
+                wait_col(0)
+                wait_col(1)
+                pan = colp.at[k]
+                cpr[...] = two(product(four(pan[...]), from_panel(lambda c: four(pan[:, :, c])), brepd, 16, spread_dia))
+
+            @pl.when(is_col)
+            def _():
+                mat[:, xk] = cpr[...]
+            wait_row(x1)
+
+            def keep(p, cols):
+                cb[p] = two(cols)
+            acc = two(product(four(mat[:, x1]), saving(from_panel(lambda c: four(cpr[:, :, c])), keep), brep.at[x1],
+                              16, spread_row(x1)))
+            mat[:, x1] = acc
+
+            @pl.when(own_col)
+            def _():
+                colp[n] = acc
+                for a in range(2):
+                    col_copy(n, a).start()
+
+            def joint(t, carry):
+                x = (x1 + 1 + t) % 4
+
+                @pl.when((col != k % 2) | (t != 2))
+                def _():
+                    wait_row(x)
+                    mat[:, x] = two(product(four(mat[:, x]), lambda g, s: four(cb[8 * g + s]), brep.at[x],
+                                            16, spread_row(x)))
+                return carry
+            lax.fori_loop(0, 3, joint, 0)
         return carry
     lax.fori_loop(0, ROUNDS, one_round, 0)
 
@@ -316,10 +394,10 @@
                 pltpu.VMEM((ROUNDS + 1, 4, 2, 8) + tile, jnp.float32),
                 pltpu.VMEM((ROUNDS + 1, 2, 2, 8) + tile, jnp.float32),
                 pltpu.VMEM((ROUNDS, 2, 8) + tile, jnp.float32),
-                pltpu.VMEM((2, BLK, 2) + tile, jnp.float32),
+                pltpu.VMEM((BLK, 2, 2) + tile, jnp.float32),
                 pltpu.VMEM((4, 16, 8) + tile, jnp.float32),
                 pltpu.VMEM((16, 8) + tile, jnp.float32),
-                pltpu.VMEM((2, 8) + tile, jnp.float32),
+                pltpu.VMEM((2, 2, 8) + tile, jnp.float32),
                 dma((ROUNDS, 4, 3)), dma((ROUNDS, 4)),
                 dma((ROUNDS, 2)), dma((ROUNDS, 2)),
                 dma((ROUNDS, 4)), dma((ROUNDS,)), dma((ROUNDS,)),

time: 89.7 us -> 91 us (1.014)
  Pallas kernels: 87.6 us -> 89 us
    pallas_call x1, Pallas kernels: 87.6 us -> 89 us  [local_run(): pl.pallas_call(kernel, out_shape=jax.ShapeDtypeStruct(local_dist.shape, l...]
where the time goes in v6:
time: 91 us; the launch traced here: 90.8 us
  Pallas kernels  89 us (98%)
  local copies, waits for them, and re-layouts  1.87 us (2%)
    pallas_call x1, Pallas kernels, local_run(): pl.pallas_call(kernel, out_shape=jax.ShapeDtypeStruct(local_dist.shape, l...  89 us
    unnamed x1, local copies, waits for them, and re-layouts  1.87 us

profile of v6, /device:TPU:1, one launch (start us, length us, event | category | flops | bytes accessed | tf_op | source)
XLA Modules:
  0.0 90.8 jit_solution(11301219035393954128)
XLA Ops:
  0.0 89.0 %apsp.1 = f32[2,128,512]{2,1,0:T(8,128)} custom-call(f32[2,128,512]{2,1,0:T(8,128)} %in_ref.1), custom_call_target="tpu_custom_call" | custom-call | tf_op jit(solution)/shard_map/apsp/pallas_call | solution.py:387
  89.0 1.9 %copy.3 = f32[2,128,512]{2,1,0:T(8,128)} copy(f32[2,128,512]{2,1,0:T(8,128)} %apsp.1) | data formatting | bytes 1048576

commit v7 on v5

--- a/solution.py
+++ b/solution.py
@@ -131,31 +131,39 @@
 
     slot_r = jnp.where(my_row == 0, 0, ROUNDS)
     slot_c = jnp.where(col == 0, 0, ROUNDS)
+    def unpack(a, x):
+        for r in range(2):
+            tiles = swap_chunks(in_ref[a, 64 * r:64 * r + 64, BLK * x:BLK * x + BLK].reshape(8, 8, 128))
+            mat[a, x, r] = tiles
+            if a == 0:
+                rowp[slot_r, x, r] = tiles
+            if x == 0:
+                colp[slot_c, a, r] = tiles
+
+    unpack(0, 0)
+
+    @pl.when((my_row == 0) & (col == 0))
+    def _():
+        close(0, 0, 0)
+        pl.semaphore_wait(barrier, 7)
+        send_dia(0)
     for a in range(2):
         for x in range(4):
-            for r in range(2):
-                tiles = swap_chunks(in_ref[a, 64 * r:64 * r + 64, BLK * x:BLK * x + BLK].reshape(8, 8, 128))
-                mat[a, x, r] = tiles
-                if a == 0:
-                    rowp[slot_r, x, r] = tiles
-                if x == 0:
-                    colp[slot_c, a, r] = tiles
-
-    pl.semaphore_wait(barrier, 7)
-
-    @pl.when((my_row == 0) & (col == 0))
+            if a + x:
+                unpack(a, x)
+
+    @pl.when((my_row != 0) | (col != 0))
     def _():
-        close_and_send(0, 0, 0)
+        pl.semaphore_wait(barrier, 7)
 
     @pl.when(my_row == 0)
     def _():
-        for x in range(4):
-            if x == 0:
-                @pl.when(col != 0)
-                def _():
-                    send_row(0, 0)
-            else:
-                send_row(0, x)
+        for x in (1, 2, 3):
+            send_row(0, x)
+
+        @pl.when(col != 0)
+        def _():
+            send_row(0, 0)
 
     @pl.when(col == 0)
     def _():
@@ -174,6 +182,16 @@
         xk = k // 2
         is_row, is_col = my_row == k % 4, col == k % 2
 
+        def first_rows():
+            @pl.when(~is_row)
+            def _():
+                row_copy(k, x1, 0).wait_recv()
+            make_brep(rowp.at[k, x1], brep.at[x1])
+
+        @pl.when(~is_col)
+        def _():
+            first_rows()
+
         @pl.when(~is_row | ~is_col)
         def _():
             dia_copy(k, 0).wait_recv()
@@ -188,8 +206,6 @@
                 row_copy(k, x, 0).wait_recv()
 
         make_brep(dst.at[k], brepd)
-        wait_row(x1)
-        make_brep(rowp.at[k, x1], brep.at[x1])
 
         def head(h, carry):
             a = jnp.where(h == 0, a1, 1 - a1)
@@ -213,6 +229,10 @@
             @pl.when(is_col)
             def _():
                 mat[a, xk] = cpr[...]
+
+                @pl.when(h == 0)
+                def _():
+                    first_rows()
 
             @pl.when(is_col & send_it)
             def _():

time: 89.7 us -> 86.7 us (0.967)
  Pallas kernels: 87.6 us -> 84.6 us
    pallas_call x1, Pallas kernels: 87.6 us -> 84.6 us  [local_run(): pl.pallas_call(kernel, out_shape=jax.ShapeDtypeStruct(local_dist.shape, l...]
where the time goes in v7:
time: 86.7 us; the launch traced here: 86.5 us
  Pallas kernels  84.6 us (98%)
  local copies, waits for them, and re-layouts  1.87 us (2%)
    pallas_call x1, Pallas kernels, local_run(): pl.pallas_call(kernel, out_shape=jax.ShapeDtypeStruct(local_dist.shape, l...  84.6 us
    unnamed x1, local copies, waits for them, and re-layouts  1.87 us

profile of v7, /device:TPU:1, one launch (start us, length us, event | category | flops | bytes accessed | tf_op | source)
XLA Modules:
  0.0 86.5 jit_solution(5610255487507274360)
XLA Ops:
  0.0 84.6 %apsp.1 = f32[2,128,512]{2,1,0:T(8,128)} custom-call(f32[2,128,512]{2,1,0:T(8,128)} %in_ref.1), custom_call_target="tpu_custom_call" | custom-call | tf_op jit(solution)/shard_map/apsp/pallas_call | solution.py:329
  84.6 1.9 %copy.3 = f32[2,128,512]{2,1,0:T(8,128)} copy(f32[2,128,512]{2,1,0:T(8,128)} %apsp.1) | data formatting | bytes 1048576

commit v8 on v7

--- a/solution.py
+++ b/solution.py
@@ -62,18 +62,18 @@
             send_sem=col_send.at[rnd, a], recv_sem=col_recv.at[rnd, a],
             device_id=peer(1, 0, 0), device_id_type=MESH)
 
-    def dia_copy(rnd, i):
+    def dia_copy(rnd, i, r):
         turn = rnd % 2
         offs = ((1, turn, 1), (1, 1 - turn, 1), (0, 1, 1), (0, 0, 1))[i]
         return pltpu.make_async_remote_copy(
-            src_ref=dst.at[rnd], dst_ref=dst.at[rnd],
-            send_sem=dia_send.at[rnd, i], recv_sem=dia_recv.at[rnd],
+            src_ref=dst.at[rnd, r], dst_ref=dst.at[rnd, r],
+            send_sem=dia_send.at[rnd, i, r], recv_sem=dia_recv.at[rnd, r],
             device_id=peer(*offs), device_id_type=MESH)
 
-    def dia_pass(rnd):
+    def dia_pass(rnd, r):
         return pltpu.make_async_remote_copy(
-            src_ref=dst.at[rnd], dst_ref=dst.at[rnd],
-            send_sem=dia_fwd.at[rnd], recv_sem=dia_recv.at[rnd],
+            src_ref=dst.at[rnd, r], dst_ref=dst.at[rnd, r],
+            send_sem=dia_fwd.at[rnd, r], recv_sem=dia_recv.at[rnd, r],
             device_id=peer(0, 0, 1), device_id_type=MESH)
 
     def passes(rnd):
@@ -85,7 +85,8 @@
 
     def send_dia(rnd):
         for i in range(4):
-            dia_copy(rnd, i).start()
+            for r in range(2):
+                dia_copy(rnd, i, r).start()
 
     def close(rnd, a, x):
         dst[rnd] = mat[a, x]
@@ -117,13 +118,14 @@
             return carry
         lax.fori_loop(0, 16, one, 0, unroll=True)
 
+    def part(i, acc, left, right, step):
+        def pivot(u, acc):
+            b = right[i * (step // 8) + lax.div(u, 8), :, pl.ds(lax.rem(u, 8), 1), :]
+            return jnp.minimum(acc, left(i * (step // 16) + lax.div(u, 16), i * step + u, lax.rem(u, 16))[:, None] + b[None])
+        return lax.fori_loop(0, step, pivot, acc, unroll=True)
+
     def product(acc, left, right, step):
-        def chunk(i, acc):
-            def pivot(u, acc):
-                b = right[i * (step // 8) + lax.div(u, 8), :, pl.ds(lax.rem(u, 8), 1), :]
-                return jnp.minimum(acc, left(i * (step // 16) + lax.div(u, 16), i * step + u, lax.rem(u, 16))[:, None] + b[None])
-            return lax.fori_loop(0, step, pivot, acc, unroll=True)
-        return lax.fori_loop(0, BLK // step, chunk, acc, unroll=step == BLK)
+        return lax.fori_loop(0, BLK // step, lambda i, acc: part(i, acc, left, right, step), acc, unroll=step == BLK)
 
     def close_and_send(rnd, a, x):
         close(rnd, a, x)
@@ -172,6 +174,29 @@
             col_copy(0, 0).start()
         col_copy(0, 1).start()
 
+    def drain(k):
+        is_row, is_col = my_row == k % 4, col == k % 2
+        for x in range(4):
+            @pl.when(is_row & (~is_col | (x != k // 2)))
+            def _():
+                for i in range(3):
+                    row_copy(k, x, i).wait_send()
+        for a in range(2):
+            @pl.when(is_col & (~is_row | (a != k // 4)))
+            def _():
+                col_copy(k, a).wait_send()
+
+        @pl.when(is_row & is_col)
+        def _():
+            for i in range(4):
+                for r in range(2):
+                    dia_copy(k, i, r).wait_send()
+
+        @pl.when(passes(k))
+        def _():
+            for r in range(2):
+                dia_pass(k, r).wait_send()
+
     def one_round(k, carry):
         n = k + 1
         more = n < ROUNDS
@@ -192,20 +217,29 @@
         def _():
             first_rows()
 
-        @pl.when(~is_row | ~is_col)
-        def _():
-            dia_copy(k, 0).wait_recv()
-
-        @pl.when(passes(k))
-        def _():
-            dia_pass(k).start()
+        @pl.when(k > 0)
+        def _():
+            drain(k - 1)
+
+        def closed_half(r):
+            @pl.when(~is_row | ~is_col)
+            def _():
+                dia_copy(k, 0, r).wait_recv()
+
+            @pl.when(passes(k))
+            def _():
+                dia_pass(k, r).start()
+
+            def one(q, carry):
+                brepd[8 * r + q] = lanes(dst[k, r], in_grp + 16 * q)
+                return carry
+            lax.fori_loop(0, 8, one, 0, unroll=True)
 
         def wait_row(x):
             @pl.when(~is_row)
             def _():
                 row_copy(k, x, 0).wait_recv()
 
-        make_brep(dst.at[k], brepd)
 
         def head(h, carry):
             a = jnp.where(h == 0, a1, 1 - a1)
@@ -217,14 +251,33 @@
             def _():
                 col_copy(k, a).wait_recv()
 
+            pan = colp.at[k, a]
+
+            def left(c, p, l):
+                return lanes(pan[:, c], grp_base + l)
+
+            @pl.when(h == 0)
+            def _():
+                @pl.when(~on_diag)
+                def _():
+                    cpr[...] = pan[...]
+
+                def by_half(r, carry):
+                    closed_half(r)
+
+                    @pl.when(~on_diag)
+                    def _():
+                        cpr[...] = part(r, cpr[...], left, brepd, BLK // 2)
+                    return carry
+                lax.fori_loop(0, 2, by_half, 0)
+
             @pl.when(on_diag)
             def _():
                 cpr[...] = dst[k]
 
-            @pl.when(~on_diag)
-            def _():
-                pan = colp.at[k, a]
-                cpr[...] = product(pan[...], lambda c, p, l: lanes(pan[:, c], grp_base + l), brepd, HEAD_STEP)
+            @pl.when(~on_diag & (h == 1))
+            def _():
+                cpr[...] = product(pan[...], left, brepd, HEAD_STEP)
 
             @pl.when(is_col)
             def _():
@@ -296,28 +349,7 @@
                 tiles = swap_chunks(mat[a, x, r])
                 out_ref[a, 64 * r:64 * r + 64, BLK * x:BLK * x + BLK] = tiles.reshape(64, 128)
 
-    def drain(k, carry):
-        is_row, is_col = my_row == k % 4, col == k % 2
-        for x in range(4):
-            @pl.when(is_row & (~is_col | (x != k // 2)))
-            def _():
-                for i in range(3):
-                    row_copy(k, x, i).wait_send()
-        for a in range(2):
-            @pl.when(is_col & (~is_row | (a != k // 4)))
-            def _():
-                col_copy(k, a).wait_send()
-
-        @pl.when(is_row & is_col)
-        def _():
-            for i in range(4):
-                dia_copy(k, i).wait_send()
-
-        @pl.when(passes(k))
-        def _():
-            dia_pass(k).wait_send()
-        return carry
-    lax.fori_loop(0, ROUNDS, drain, 0)
+    drain(ROUNDS - 1)
 
 
 def solution(mesh):
@@ -342,7 +374,7 @@
                 pltpu.VMEM((2, 8) + tile, jnp.float32),
                 dma((ROUNDS, 4, 3)), dma((ROUNDS, 4)),
                 dma((ROUNDS, 2)), dma((ROUNDS, 2)),
-                dma((ROUNDS, 4)), dma((ROUNDS,)), dma((ROUNDS,)),
+                dma((ROUNDS, 4, 2)), dma((ROUNDS, 2)), dma((ROUNDS, 2)),
             ],
             compiler_params=pltpu.CompilerParams(collective_id=0, has_side_effects=True),
             name='apsp',

time: 86.7 us -> 87.1 us (level)
  no operation moved by 1% of the time
where the time goes in v8:
time: 87.1 us; the launch traced here: 86.9 us
  Pallas kernels  85 us (98%)
  local copies, waits for them, and re-layouts  1.87 us (2%)
    pallas_call x1, Pallas kernels, local_run(): pl.pallas_call(kernel, out_shape=jax.ShapeDtypeStruct(local_dist.shape, l...  85 us
    unnamed x1, local copies, waits for them, and re-layouts  1.87 us

profile of v8, /device:TPU:1, one launch (start us, length us, event | category | flops | bytes accessed | tf_op | source)
XLA Modules:
  0.0 86.9 jit_solution(15665530493665107165)
XLA Ops:
  0.0 85.0 %apsp.1 = f32[2,128,512]{2,1,0:T(8,128)} custom-call(f32[2,128,512]{2,1,0:T(8,128)} %in_ref.1), custom_call_target="tpu_custom_call" | custom-call | tf_op jit(solution)/shard_map/apsp/pallas_call | solution.py:361
  85.0 1.9 %copy.3 = f32[2,128,512]{2,1,0:T(8,128)} copy(f32[2,128,512]{2,1,0:T(8,128)} %apsp.1) | data formatting | bytes 1048576

commit v9 on v7

--- a/solution.py
+++ b/solution.py
@@ -262,14 +262,13 @@
             def _():
                 close_and_send(n, a, x1)
             return carry
-        lax.fori_loop(0, 2, head, 0)
-
-        def tail(t, carry):
+
+        def tail(phase, t, carry):
             h = t // 3
             a = jnp.where(h == 0, a1, 1 - a1)
             x = (x1 + 1 + t % 3) % 4
 
-            @pl.when((col != k % 2) | (t % 3 != 2))
+            @pl.when(((col != k % 2) | (t % 3 != 2)) & ((own_row & (h == phase)) | (~own_row & (phase == 1))))
             def _():
                 @pl.when(h == 0)
                 def _():
@@ -286,7 +285,10 @@
                 def _():
                     send_row(n, x)
             return carry
-        lax.fori_loop(0, 6, tail, 0)
+        def in_order(phase, carry):
+            head(phase, carry)
+            return lax.fori_loop(0, 6, functools.partial(tail, phase), carry)
+        lax.fori_loop(0, 2, in_order, 0)
         return carry
     lax.fori_loop(0, ROUNDS, one_round, 0)
 

time: 86.7 us -> 84.7 us (0.977)
  Pallas kernels: 84.6 us -> 82.6 us
    pallas_call x1, Pallas kernels: 84.6 us -> 82.6 us  [local_run(): pl.pallas_call(kernel, out_shape=jax.ShapeDtypeStruct(local_dist.shape, l...]
where the time goes in v9:
time: 84.7 us; the launch traced here: 84.5 us
  Pallas kernels  82.6 us (98%)
  local copies, waits for them, and re-layouts  1.87 us (2%)
    pallas_call x1, Pallas kernels, local_run(): pl.pallas_call(kernel, out_shape=jax.ShapeDtypeStruct(local_dist.shape, l...  82.6 us
    unnamed x1, local copies, waits for them, and re-layouts  1.87 us

profile of v9, /device:TPU:1, one launch (start us, length us, event | category | flops | bytes accessed | tf_op | source)
XLA Modules:
  0.0 84.5 jit_solution(14435157741501736307)
XLA Ops:
  0.0 82.6 %apsp.1 = f32[2,128,512]{2,1,0:T(8,128)} custom-call(f32[2,128,512]{2,1,0:T(8,128)} %in_ref.1), custom_call_target="tpu_custom_call" | custom-call | tf_op jit(solution)/shard_map/apsp/pallas_call | solution.py:331
  82.6 1.9 %copy.3 = f32[2,128,512]{2,1,0:T(8,128)} copy(f32[2,128,512]{2,1,0:T(8,128)} %apsp.1) | data formatting | bytes 1048576

commit v10 on v9

--- a/solution.py
+++ b/solution.py
@@ -346,7 +346,7 @@
                 dma((ROUNDS, 2)), dma((ROUNDS, 2)),
                 dma((ROUNDS, 4)), dma((ROUNDS,)), dma((ROUNDS,)),
             ],
-            compiler_params=pltpu.CompilerParams(collective_id=0, has_side_effects=True),
+            compiler_params=pltpu.CompilerParams(collective_id=0, has_side_effects=True, vmem_limit_bytes=16 * 2 ** 20),
             name='apsp',
         )(local_dist)
 

time: 84.7 us -> 82.7 us (0.976)
  Pallas kernels: 82.6 us -> 80.8 us
    pallas_call x1, Pallas kernels: 82.6 us -> 80.8 us  [local_run(): pl.pallas_call(kernel, out_shape=jax.ShapeDtypeStruct(local_dist.shape, l...]
    unnamed x1 -> x3, local copies, waits for them, and re-layouts: 1.87 us -> 1.84 us
where the time goes in v10:
time: 82.7 us; the launch traced here: 82.6 us
  Pallas kernels  80.8 us (98%)
  local copies, waits for them, and re-layouts  1.84 us (2%)
    pallas_call x1, Pallas kernels, local_run(): pl.pallas_call(kernel, out_shape=jax.ShapeDtypeStruct(local_dist.shape, l...  80.8 us
    unnamed x3, local copies, waits for them, and re-layouts  1.84 us

profile of v10, /device:TPU:1, one launch (start us, length us, event | category | flops | bytes accessed | tf_op | source)
XLA Modules:
  0.0 82.6 jit_solution(13914472779779042458)
XLA Ops:
  0.0 0.0 copy-start
  0.0 1.0 %copy-done = f32[2,128,512]{2,1,0:T(8,128)S(1)} copy-done((f32[2,128,512]{2,1,0:T(8,128)S(1)}, f32[2,128,512]{2,1,0:T(8,128)}, u32[]{:S(2)}) %copy-start) | copy-done | bytes 524312
  1.0 80.8 %apsp.1 = f32[2,128,512]{2,1,0:T(8,128)S(1)} custom-call(f32[2,128,512]{2,1,0:T(8,128)S(1)} %copy-done), custom_call_target="tpu_custom_call" | custom-call | tf_op jit(solution)/shard_map/apsp/pallas_call | solution.py:331
  81.8 0.8 copy.3
Async XLA Ops:
  0.0 1.0 %copy-start = (f32[2,128,512]{2,1,0:T(8,128)S(1)}, f32[2,128,512]{2,1,0:T(8,128)}, u32[]{:S(2)}) copy-start(f32[2,128,512]{2,1,0:T(8,128)} %in_ref.1) | copy-start | bytes 1572868

commit v11 on v10

--- a/solution.py
+++ b/solution.py
@@ -21,7 +21,7 @@
     return jnp.take_along_axis(flat, idx, axis=1, mode='promise_in_bounds').reshape(tiles.shape)
 
 
-def kernel(in_ref, out_ref, mat, rowp, colp, dst, cb, brep, brepd, cpr,
+def kernel(src_ref, out_ref, in_ref, in_sem, mat, rowp, colp, dst, cb, brep, brepd, cpr,
 
            row_send, row_recv, col_send, col_recv, dia_send, dia_fwd, dia_recv):
     row, sub, col = lax.axis_index('row'), lax.axis_index('sub'), lax.axis_index('col')
@@ -37,6 +37,8 @@
     barrier = pltpu.get_barrier_semaphore()
     for offs in ALL_PEERS:
         pl.semaphore_signal(barrier, inc=1, device_id=peer(*offs), device_id_type=MESH)
+    fetch = pltpu.make_async_copy(src_ref, in_ref, in_sem)
+    fetch.start()
 
     def swap_chunks(tiles):
         for bit in (1, 2, 4):
@@ -140,6 +142,7 @@
             if x == 0:
                 colp[slot_c, a, r] = tiles
 
+    fetch.wait()
     unpack(0, 0)
 
     @pl.when((my_row == 0) & (col == 0))
@@ -331,9 +334,10 @@
         return pl.pallas_call(
             kernel,
             out_shape=jax.ShapeDtypeStruct(local_dist.shape, local_dist.dtype),
-            in_specs=[pl.BlockSpec(memory_space=pltpu.VMEM)],
+            in_specs=[pl.BlockSpec(memory_space=pltpu.HBM)],
             out_specs=pl.BlockSpec(memory_space=pltpu.VMEM),
             scratch_shapes=[
+                pltpu.VMEM(local_dist.shape, jnp.float32), dma(()),
                 pltpu.VMEM((2, 4, 2, 8) + tile, jnp.float32),
                 pltpu.VMEM((ROUNDS + 1, 4, 2, 8) + tile, jnp.float32),
                 pltpu.VMEM((ROUNDS + 1, 2, 2, 8) + tile, jnp.float32),
@@ -346,7 +350,7 @@
                 dma((ROUNDS, 2)), dma((ROUNDS, 2)),
                 dma((ROUNDS, 4)), dma((ROUNDS,)), dma((ROUNDS,)),
             ],
-            compiler_params=pltpu.CompilerParams(collective_id=0, has_side_effects=True, vmem_limit_bytes=16 * 2 ** 20),
+            compiler_params=pltpu.CompilerParams(collective_id=0, has_side_effects=True, vmem_limit_bytes=55839744),
             name='apsp',
         )(local_dist)
 

time: 82.7 us -> 82.7 us (level)
  local copies, waits for them, and re-layouts: 1.84 us -> 0.8 us
  Pallas kernels: 80.8 us -> 81.8 us
    unnamed x3 -> x1, local copies, waits for them, and re-layouts: 1.84 us -> 0.8 us
    pallas_call x1, Pallas kernels: 80.8 us -> 81.8 us  [local_run(): pl.pallas_call(kernel, out_shape=jax.ShapeDtypeStruct(local_dist.shape, l...]
where the time goes in v11:
time: 82.7 us; the launch traced here: 82.6 us
  Pallas kernels  81.8 us (99%)
    pallas_call x1, Pallas kernels, local_run(): pl.pallas_call(kernel, out_shape=jax.ShapeDtypeStruct(local_dist.shape, l...  81.8 us

profile of v11, /device:TPU:1, one launch (start us, length us, event | category | flops | bytes accessed | tf_op | source)
XLA Modules:
  0.0 82.6 jit_solution(15967530558840390326)
XLA Ops:
  0.0 81.8 %apsp.1 = f32[2,128,512]{2,1,0:T(8,128)S(1)} custom-call(f32[2,128,512]{2,1,0:T(8,128)} %src_ref.1), custom_call_target="tpu_custom_call" | custom-call | tf_op jit(solution)/shard_map/apsp/pallas_call | solution.py:334
  81.8 0.8 copy.3

commit v12 on v11

--- a/solution.py
+++ b/solution.py
@@ -175,6 +175,27 @@
             col_copy(0, 0).start()
         col_copy(0, 1).start()
 
+    def drain(k):
+        is_row, is_col = my_row == k % 4, col == k % 2
+        for x in range(4):
+            @pl.when(is_row & (~is_col | (x != k // 2)))
+            def _():
+                for i in range(3):
+                    row_copy(k, x, i).wait_send()
+        for a in range(2):
+            @pl.when(is_col & (~is_row | (a != k // 4)))
+            def _():
+                col_copy(k, a).wait_send()
+
+        @pl.when(is_row & is_col)
+        def _():
+            for i in range(4):
+                dia_copy(k, i).wait_send()
+
+        @pl.when(passes(k))
+        def _():
+            dia_pass(k).wait_send()
+
     def one_round(k, carry):
         n = k + 1
         more = n < ROUNDS
@@ -194,6 +215,10 @@
         @pl.when(~is_col)
         def _():
             first_rows()
+
+        @pl.when(k > 0)
+        def _():
+            drain(k - 1)
 
         @pl.when(~is_row | ~is_col)
         def _():
@@ -301,28 +326,7 @@
                 tiles = swap_chunks(mat[a, x, r])
                 out_ref[a, 64 * r:64 * r + 64, BLK * x:BLK * x + BLK] = tiles.reshape(64, 128)
 
-    def drain(k, carry):
-        is_row, is_col = my_row == k % 4, col == k % 2
-        for x in range(4):
-            @pl.when(is_row & (~is_col | (x != k // 2)))
-            def _():
-                for i in range(3):
-                    row_copy(k, x, i).wait_send()
-        for a in range(2):
-            @pl.when(is_col & (~is_row | (a != k // 4)))
-            def _():
-                col_copy(k, a).wait_send()
-
-        @pl.when(is_row & is_col)
-        def _():
-            for i in range(4):
-                dia_copy(k, i).wait_send()
-
-        @pl.when(passes(k))
-        def _():
-            dia_pass(k).wait_send()
-        return carry
-    lax.fori_loop(0, ROUNDS, drain, 0)
+    drain(ROUNDS - 1)
 
 
 def solution(mesh):

time: 82.7 us -> 82.6 us (level)
  no operation moved by 1% of the time
where the time goes in v12:
time: 82.6 us; the launch traced here: 82.5 us
  Pallas kernels  81.7 us (99%)
    pallas_call x1, Pallas kernels, local_run(): pl.pallas_call(kernel, out_shape=jax.ShapeDtypeStruct(local_dist.shape, l...  81.7 us

profile of v12, /device:TPU:1, one launch (start us, length us, event | category | flops | bytes accessed | tf_op | source)
XLA Modules:
  0.0 82.5 jit_solution(12156258314689395741)
XLA Ops:
  0.0 81.7 %apsp.1 = f32[2,128,512]{2,1,0:T(8,128)S(1)} custom-call(f32[2,128,512]{2,1,0:T(8,128)} %src_ref.1), custom_call_target="tpu_custom_call" | custom-call | tf_op jit(solution)/shard_map/apsp/pallas_call | solution.py:338
  81.7 0.8 copy.3

commit v13 on v12

--- a/solution.py
+++ b/solution.py
@@ -127,6 +127,17 @@
             return lax.fori_loop(0, step, pivot, acc, unroll=True)
         return lax.fori_loop(0, BLK // step, chunk, acc, unroll=step == BLK)
 
+    def product_spreading(acc, tab, src, out):
+        def half(r, acc):
+            def group(q, acc):
+                g = 8 * r + q
+                out[g] = lanes(src[r], in_grp + 16 * q)
+                for s in range(8):
+                    acc = jnp.minimum(acc, tab[8 * g + s][:, None] + out[g, :, s:s + 1, :][None])
+                return acc
+            return lax.fori_loop(0, 8, group, acc, unroll=True)
+        return lax.fori_loop(0, 2, half, acc)
+
     def close_and_send(rnd, a, x):
         close(rnd, a, x)
         send_dia(rnd)
@@ -298,19 +309,20 @@
 
             @pl.when(((col != k % 2) | (t % 3 != 2)) & ((own_row & (h == phase)) | (~own_row & (phase == 1))))
             def _():
+                tab = cb.at[a]
+
                 @pl.when(h == 0)
                 def _():
                     wait_row(x)
-                    make_brep(rowp.at[k, x], brep.at[x])
-
-                tab = cb.at[a]
-                acc = product(mat[a, x], lambda c, p, l: tab[p], brep.at[x], TAIL_STEP)
-                mat[a, x] = acc
-                send_it = own_row & (h == 0)
-                rowp[jnp.where(send_it, n, ROUNDS), x] = acc
-
-                @pl.when(send_it)
+                    mat[a, x] = product_spreading(mat[a, x], tab, rowp.at[k, x], brep.at[x])
+
+                @pl.when(h == 1)
                 def _():
+                    mat[a, x] = product(mat[a, x], lambda c, p, l: tab[p], brep.at[x], TAIL_STEP)
+
+                @pl.when(own_row & (h == 0))
+                def _():
+                    rowp[n, x] = mat[a, x]
                     send_row(n, x)
             return carry
         def in_order(phase, carry):

time: 82.6 us -> 81.2 us (0.983)
  Pallas kernels: 81.7 us -> 80.2 us
    pallas_call x1, Pallas kernels: 81.7 us -> 80.2 us  [local_run(): pl.pallas_call(kernel, out_shape=jax.ShapeDtypeStruct(local_dist.shape, l...]
where the time goes in v13:
time: 81.2 us; the launch traced here: 81 us
  Pallas kernels  80.2 us (99%)
    pallas_call x1, Pallas kernels, local_run(): pl.pallas_call(kernel, out_shape=jax.ShapeDtypeStruct(local_dist.shape, l...  80.2 us

profile of v13, /device:TPU:1, one launch (start us, length us, event | category | flops | bytes accessed | tf_op | source)
XLA Modules:
  0.0 81.0 jit_solution(18120910711042287176)
XLA Ops:
  0.0 80.2 %apsp.1 = f32[2,128,512]{2,1,0:T(8,128)S(1)} custom-call(f32[2,128,512]{2,1,0:T(8,128)} %src_ref.1), custom_call_target="tpu_custom_call" | custom-call | tf_op jit(solution)/shard_map/apsp/pallas_call | solution.py:350
  80.2 0.8 copy.3

commit v14 on v13

--- a/solution.py
+++ b/solution.py
@@ -172,12 +172,11 @@
 
     @pl.when(my_row == 0)
     def _():
+        @pl.when(col != 0)
+        def _():
+            send_row(0, 0)
         for x in (1, 2, 3):
             send_row(0, x)
-
-        @pl.when(col != 0)
-        def _():
-            send_row(0, 0)
 
     @pl.when(col == 0)
     def _():

time: 81.2 us -> 78.5 us (0.967)
  Pallas kernels: 80.2 us -> 77.6 us
    pallas_call x1, Pallas kernels: 80.2 us -> 77.6 us  [local_run(): pl.pallas_call(kernel, out_shape=jax.ShapeDtypeStruct(local_dist.shape, l...]
where the time goes in v14:
time: 78.5 us; the launch traced here: 78.4 us
  Pallas kernels  77.6 us (99%)
  local copies, waits for them, and re-layouts  0.8 us (1%)
    pallas_call x1, Pallas kernels, local_run(): pl.pallas_call(kernel, out_shape=jax.ShapeDtypeStruct(local_dist.shape, l...  77.6 us

profile of v14, /device:TPU:1, one launch (start us, length us, event | category | flops | bytes accessed | tf_op | source)
XLA Modules:
  0.0 78.4 jit_solution(6096055776733366194)
XLA Ops:
  0.0 77.6 %apsp.1 = f32[2,128,512]{2,1,0:T(8,128)S(1)} custom-call(f32[2,128,512]{2,1,0:T(8,128)} %src_ref.1), custom_call_target="tpu_custom_call" | custom-call | tf_op jit(solution)/shard_map/apsp/pallas_call | solution.py:349
  77.6 0.8 %copy.3 = f32[2,128,512]{2,1,0:T(8,128)} copy(f32[2,128,512]{2,1,0:T(8,128)S(1)} %apsp.1) | data formatting | bytes 1048576

commit v15 on v14

--- a/solution.py
+++ b/solution.py
@@ -275,7 +275,6 @@
             @pl.when(is_col & send_it)
             def _():
                 rowp[n, xk] = cpr[...]
-                send_row(n, xk)
 
             tab = cb.at[a]
 
@@ -326,7 +325,12 @@
             return carry
         def in_order(phase, carry):
             head(phase, carry)
-            return lax.fori_loop(0, 6, functools.partial(tail, phase), carry)
+            lax.fori_loop(0, 6, functools.partial(tail, phase), 0)
+
+            @pl.when(is_col & own_row & (phase == 0))
+            def _():
+                send_row(n, xk)
+            return carry
         lax.fori_loop(0, 2, in_order, 0)
         return carry
     lax.fori_loop(0, ROUNDS, one_round, 0)

time: 78.5 us -> 77.8 us (level)
  Pallas kernels: 77.6 us -> 76.8 us
where the time goes in v15:
time: 77.8 us; the launch traced here: 77.7 us
  Pallas kernels  76.8 us (99%)
  local copies, waits for them, and re-layouts  0.8 us (1%)
    pallas_call x1, Pallas kernels, local_run(): pl.pallas_call(kernel, out_shape=jax.ShapeDtypeStruct(local_dist.shape, l...  76.8 us

profile of v15, /device:TPU:1, one launch (start us, length us, event | category | flops | bytes accessed | tf_op | source)
XLA Modules:
  0.0 77.7 jit_solution(399706663354537509)
XLA Ops:
  0.0 76.8 %apsp.1 = f32[2,128,512]{2,1,0:T(8,128)S(1)} custom-call(f32[2,128,512]{2,1,0:T(8,128)} %src_ref.1), custom_call_target="tpu_custom_call" | custom-call | tf_op jit(solution)/shard_map/apsp/pallas_call | solution.py:353
  76.9 0.8 %copy.3 = f32[2,128,512]{2,1,0:T(8,128)} copy(f32[2,128,512]{2,1,0:T(8,128)S(1)} %apsp.1) | data formatting | bytes 1048576
